TPU v7x, 32 devices: a whole 2x2x4 slice. The times are simulated.
32 devices in a mesh: ma: 8 (over z, x), band: 4 (over y, core).
Axes of the slice: x: 2, y: 2, z: 4, core: 2. Of those that a mesh axis runs over, the one named last changes fastest.
Arguments:
- observed: bfloat16 [256, 64, 1024], P(('ma', 'band')), may hold values from -6 to 6
- eigenvalues: float32 [256, 1024], P(('ma', 'band')), may hold values from 0.05 to 20
- kl_basis: bfloat16 [256, 1024, 512], P(('ma', 'band')), may hold values from -0.1875 to 0.1875
- band_deriv: bfloat16 [40, 512, 512], P('band'), may hold values from -0.15625 to 0.15625, as said below
- counts: int32 [256], P(('ma', 'band')), may hold values from 128 to 1024, as said below
Outputs:
- mode_power: float32 [256, 40], P('ma', 'band')
- band_power: float32 [40], P('band')
Inputs may be any that keep to these rules, and one draw needn't show every extreme that they name: counts[m] is the number of leading KL modes of m-mode m that are kept; some m-mode keeps 1024 and some keeps 1024 // 8. Each band_deriv[a] is symmetric.
All inputs are finite; a program needn't handle non-finite values.
Results may differ from a plain program's by a relative error of at most 0.0018.
Values may be sent and summed in bfloat16 or wider, within the bound.
No kernel may reach another device: no remote copies, remote signals or barrier semaphores. Data moves between devices by JAX's collectives and lax.ppermute only.
A program may use at most 64 MiB of HBM per device.

v0:
```python
import jax
import jax.numpy as jnp
from jax import lax
from jax.sharding import PartitionSpec as P


def weigh(observed, eigenvalues, counts):
    position = lax.broadcasted_iota(jnp.int32, eigenvalues.shape, 1)
    inside = position < counts[:, None]
    weights = jnp.where(inside, 1.0 / (1.0 + eigenvalues), jnp.zeros_like(eigenvalues))
    return (observed.astype(jnp.float32) * weights[:, None, :]).astype(jnp.bfloat16)


def project_padded(weighted, kl_basis):
    return jnp.einsum("msi,miw->msw", weighted, kl_basis, preferred_element_type=jnp.float32)


def band_quadratic(vectors, matrices):
    mode_count = vectors.shape[0]
    flattened = vectors.reshape(mode_count * vectors.shape[1], vectors.shape[2])

    def one_band(matrix):
        mapped = jnp.dot(flattened, matrix, preferred_element_type=jnp.float32)
        return jnp.sum((mapped * flattened).reshape(mode_count, -1), axis=1)

    return lax.map(one_band, matrices)


def per_device(observed, eigenvalues, kl_basis, band_deriv, counts):
    samples = observed.shape[1]
    live_total = lax.psum(jnp.sum(counts).astype(jnp.float32), ("ma", "band"))
    weighted = weigh(observed, eigenvalues, counts)
    projected = project_padded(weighted, kl_basis)
    projected = projected.astype(jnp.bfloat16)
    quadratic = band_quadratic(lax.all_gather(projected, "band", axis=0, tiled=True), band_deriv)
    mode_power = jnp.transpose(quadratic) / samples
    partial_sum = jnp.sum(mode_power, axis=0)
    band_total = lax.psum(partial_sum, "ma")
    band_power = observed.shape[2] * band_total / live_total
    return (mode_power, band_power)


def solution(mesh):
    in_specs = (
        P(("ma", "band"), None, None),
        P(("ma", "band"), None),
        P(("ma", "band"), None, None),
        P("band", None, None),
        P(("ma", "band")),
    )
    out_specs = (P("ma", "band"), P("band"))
    return jax.shard_map(
        per_device, mesh=mesh, in_specs=in_specs, out_specs=out_specs, check_vma=False
    )
```

profile of v0, /device:TPU:0, one launch (start us, length us, event | category | flops | bytes accessed | tf_op | source)
XLA Modules:
  0.0 117.1 jit_solution(10019816696674286477)
XLA Ops:
  7.2 0.8 divide_select_fusion
  8.0 6.0 %convolution_convert_fusion = bf16[8,64,512]{2,1,0:T(8,128)(2,1)} fusion(bf16[8,1024,512]{2,1,0:T(8,128)(2,1)} %param.9, bf16[8,64,1024]{2,1,0:T(8,128)(2,1)} %param.7, f32[8,1024]{1,0:T(8,128)S(1)} %divide_select_fusion), kind=kOutput, calls=%fused_computation.6 | convolution fusion | flops 538705920 | bytes 9994240 | tf_op jit(solution)/shard_map/msi,miw->msw/dot_general | solution.py:15
  14.1 0.6 reduce_sum.35
  15.4 42.4 %psum.15 = f32[]{:T(128)} all-reduce(f32[]{:T(128)S(6)} %convert_element_type.18), channel_id=1, replica_groups=mesh['ma'=8,'band'=4] {'ma','band'}, use_global_device_ids=true, to_apply=%region_7.8 | all-reduce | flops 1 | bytes 8 | tf_op jit(solution)/shard_map/psum | solution.py:31
  57.8 2.9 %copy.9 = bf16[2048,512]{0,1:T(8,128)(2,1)S(1)} copy(bf16[2048,512]{1,0:T(8,128)(2,1)} %bitcast.21) | data formatting | bytes 4194304 | tf_op jit(solution)/shard_map/while | solution.py:26
  60.8 26.6 %while.10 = (s32[]{:T(128)}, f32[10,32]{1,0:T(8,128)S(1)}, bf16[10,512,512]{2,1,0:T(8,128)(2,1)}, bf16[2048,512]{0,1:T(8,128)(2,1)S(1)}, s32[]{:T(128)}, /*index=5*/f32[]{:T(128)}, s32[]{:T(128)}) while((s32[]{:T(128)}, f32[10,32]{1,0:T(8,128)S(1)}, bf16[10,512,512]{2,1,0:T(8,128)(2,1)}, bf16[2048,512]{0,1:T(8,128)(2,1)S(1)}, s32[]{:T(128)}, ...), condition=%wide.region_3.4_spmd, body=%wide.region_0.3_spmd.sunk | while | flops 1076887552 | bytes 4752341 | solution.py:26
  60.8 2.4 %fusion.12 = f32[2048]{0:T(1024)S(1)} fusion(bf16[2048,512]{0,1:T(8,128)(2,1)S(1)} %get-tuple-element.89, bf16[10,512,512]{2,1,0:T(8,128)(2,1)} %get-tuple-element.88, s32[]{:T(128)} %get-tuple-element.79), kind=kOutput, calls=%fused_computation.1.clone.1 | convolution fusion | flops 1076885504 | bytes 4727296 | tf_op jit(solution)/shard_map/while/body/eval_jaxpr/dot_general | solution.py:23
  63.2 0.1 reduce_sum.42
  63.3 0.1 reduce_sum.43
  63.4 2.4 %fusion.12 = f32[2048]{0:T(1024)S(1)} fusion(bf16[2048,512]{0,1:T(8,128)(2,1)S(1)} %get-tuple-element.89, bf16[10,512,512]{2,1,0:T(8,128)(2,1)} %get-tuple-element.88, s32[]{:T(128)} %get-tuple-element.79), kind=kOutput, calls=%fused_computation.1.clone.1 | convolution fusion | flops 1076885504 | bytes 4727296 | tf_op jit(solution)/shard_map/while/body/eval_jaxpr/dot_general | solution.py:23
  65.9 0.1 reduce_sum.42
  65.9 0.1 reduce_sum.43
  66.1 2.4 %fusion.12 = f32[2048]{0:T(1024)S(1)} fusion(bf16[2048,512]{0,1:T(8,128)(2,1)S(1)} %get-tuple-element.89, bf16[10,512,512]{2,1,0:T(8,128)(2,1)} %get-tuple-element.88, s32[]{:T(128)} %get-tuple-element.79), kind=kOutput, calls=%fused_computation.1.clone.1 | convolution fusion | flops 1076885504 | bytes 4727296 | tf_op jit(solution)/shard_map/while/body/eval_jaxpr/dot_general | solution.py:23
  68.5 0.1 reduce_sum.42
  68.6 0.1 reduce_sum.43
  68.7 2.4 %fusion.12 = f32[2048]{0:T(1024)S(1)} fusion(bf16[2048,512]{0,1:T(8,128)(2,1)S(1)} %get-tuple-element.89, bf16[10,512,512]{2,1,0:T(8,128)(2,1)} %get-tuple-element.88, s32[]{:T(128)} %get-tuple-element.79), kind=kOutput, calls=%fused_computation.1.clone.1 | convolution fusion | flops 1076885504 | bytes 4727296 | tf_op jit(solution)/shard_map/while/body/eval_jaxpr/dot_general | solution.py:23
  71.2 0.1 reduce_sum.43
  71.4 2.4 %fusion.12 = f32[2048]{0:T(1024)S(1)} fusion(bf16[2048,512]{0,1:T(8,128)(2,1)S(1)} %get-tuple-element.89, bf16[10,512,512]{2,1,0:T(8,128)(2,1)} %get-tuple-element.88, s32[]{:T(128)} %get-tuple-element.79), kind=kOutput, calls=%fused_computation.1.clone.1 | convolution fusion | flops 1076885504 | bytes 4727296 | tf_op jit(solution)/shard_map/while/body/eval_jaxpr/dot_general | solution.py:23
  73.9 0.1 reduce_sum.43
  74.1 2.4 %fusion.12 = f32[2048]{0:T(1024)S(1)} fusion(bf16[2048,512]{0,1:T(8,128)(2,1)S(1)} %get-tuple-element.89, bf16[10,512,512]{2,1,0:T(8,128)(2,1)} %get-tuple-element.88, s32[]{:T(128)} %get-tuple-element.79), kind=kOutput, calls=%fused_computation.1.clone.1 | convolution fusion | flops 1076885504 | bytes 4727296 | tf_op jit(solution)/shard_map/while/body/eval_jaxpr/dot_general | solution.py:23
  76.5 0.1 reduce_sum.43
  76.7 2.4 %fusion.12 = f32[2048]{0:T(1024)S(1)} fusion(bf16[2048,512]{0,1:T(8,128)(2,1)S(1)} %get-tuple-element.89, bf16[10,512,512]{2,1,0:T(8,128)(2,1)} %get-tuple-element.88, s32[]{:T(128)} %get-tuple-element.79), kind=kOutput, calls=%fused_computation.1.clone.1 | convolution fusion | flops 1076885504 | bytes 4727296 | tf_op jit(solution)/shard_map/while/body/eval_jaxpr/dot_general | solution.py:23
  79.2 0.1 reduce_sum.43
  79.4 2.4 %fusion.12 = f32[2048]{0:T(1024)S(1)} fusion(bf16[2048,512]{0,1:T(8,128)(2,1)S(1)} %get-tuple-element.89, bf16[10,512,512]{2,1,0:T(8,128)(2,1)} %get-tuple-element.88, s32[]{:T(128)} %get-tuple-element.79), kind=kOutput, calls=%fused_computation.1.clone.1 | convolution fusion | flops 1076885504 | bytes 4727296 | tf_op jit(solution)/shard_map/while/body/eval_jaxpr/dot_general | solution.py:23
  81.9 0.1 reduce_sum.43
  82.0 2.4 %fusion.12 = f32[2048]{0:T(1024)S(1)} fusion(bf16[2048,512]{0,1:T(8,128)(2,1)S(1)} %get-tuple-element.89, bf16[10,512,512]{2,1,0:T(8,128)(2,1)} %get-tuple-element.88, s32[]{:T(128)} %get-tuple-element.79), kind=kOutput, calls=%fused_computation.1.clone.1 | convolution fusion | flops 1076885504 | bytes 4727296 | tf_op jit(solution)/shard_map/while/body/eval_jaxpr/dot_general | solution.py:23
  84.5 0.1 reduce_sum.43
  84.7 2.4 %fusion.12 = f32[2048]{0:T(1024)S(1)} fusion(bf16[2048,512]{0,1:T(8,128)(2,1)S(1)} %get-tuple-element.89, bf16[10,512,512]{2,1,0:T(8,128)(2,1)} %get-tuple-element.88, s32[]{:T(128)} %get-tuple-element.79), kind=kOutput, calls=%fused_computation.1.clone.1 | convolution fusion | flops 1076885504 | bytes 4727296 | tf_op jit(solution)/shard_map/while/body/eval_jaxpr/dot_general | solution.py:23
  87.2 0.1 reduce_sum.43
  87.3 0.7 multiply_reduce_fusion
  88.0 21.1 %psum.14 = f32[10]{0:T(128)S(1)} all-reduce(f32[10]{0:T(128)S(1)} %get-tuple-element.45), channel_id=1, replica_groups=mesh['ma'=8,'band'=4] {'ma'}, use_global_device_ids=true, to_apply=%region_5.6 | all-reduce | flops 10 | bytes 80 | tf_op jit(solution)/shard_map/psum | solution.py:38
  109.1 1.1 multiply_divide_fusion
  (23 shorter events, 0.9 us)
Async XLA Ops:
  7.2 50.7 %all-gather.2.cloned.1.call-start = ((), (), s32[]{:S(2)}) async-start(), calls=%async_computation | async-start | bytes 2621440 | tf_op jit(solution)/shard_map/all_gather | solution.py:35
  8.0 6.1 %copy-start = (s32[8]{0:T(128)S(1)}, s32[8]{0:T(128)}, u32[]{:S(2)}) copy-start(s32[8]{0:T(128)} %param.11) | copy-start | bytes 100
Sparse Core Ops, SparseCore 0:
  14.2 25.4 all-gather.1
where the time goes:
time: 118 us; the launch traced here: 117 us
  blocking collectives  63.5 us (54%)
  matrix products  30.2 us (26%)
  between operations  14.7 us (12%)
  other arithmetic  4.47 us (4%)
  local copies, waits for them, and re-layouts  3.98 us (3%)
    psum x1, blocking collectives, per_device(): live_total = lax.psum(jnp.sum(counts).astype(jnp.float32), ('ma', 'band'))  42.4 us
    dot_general x10, matrix products, one_band(): mapped = jnp.dot(flattened, matrix, preferred_element_type=jnp.float32)  24.1 us
    psum x1, blocking collectives, per_device(): band_total = lax.psum(partial_sum, 'ma')  21.1 us
    dot_general x1, matrix products, project_padded(): jnp.einsum('msi,miw->msw', weighted, kl_basis, preferred_element_type=jnp...  6.04 us
    while x1, local copies, waits for them, and re-layouts, band_quadratic(): return lax.map(one_band, matrices)  2.93 us
  transfers between devices with their start and end apart: 1, of which 0 were waited for; matrix products, arithmetic and copies ran while one was open for 1% of the time, Pallas kernels for 0%

commit v1 on v0

--- a/solution.py
+++ b/solution.py
@@ -28,7 +28,9 @@
 
 def per_device(observed, eigenvalues, kl_basis, band_deriv, counts):
     samples = observed.shape[1]
-    live_total = lax.psum(jnp.sum(counts).astype(jnp.float32), ("ma", "band"))
+    live_total = jnp.sum(
+        lax.all_gather(jnp.sum(counts).astype(jnp.float32), ("ma", "band")), axis=0
+    )
     weighted = weigh(observed, eigenvalues, counts)
     projected = project_padded(weighted, kl_basis)
     projected = projected.astype(jnp.bfloat16)

time: 118 us -> 118 us (level)
    psum x1 -> x0, blocking collectives: 42.4 us -> none  [per_device(): live_total = lax.psum(jnp.sum(counts).astype(jnp.float32), ('ma', 'band'))]
    unnamed x0 -> x1, blocking collectives: none -> 42.2 us
where the time goes in v1:
time: 118 us
  blocking collectives  63.3 us (54%)
  matrix products  30.1 us (26%)
  between operations  14.7 us (12%)
  other arithmetic  5.07 us (4%)
  local copies, waits for them, and re-layouts  4.1 us (3%)
    unnamed x1, blocking collectives  42.2 us
    dot_general x10, matrix products, one_band(): mapped = jnp.dot(flattened, matrix, preferred_element_type=jnp.float32)  24.1 us
    psum x1, blocking collectives, per_device(): band_total = lax.psum(partial_sum, 'ma')  21.1 us
    dot_general x1, matrix products, project_padded(): jnp.einsum('msi,miw->msw', weighted, kl_basis, preferred_element_type=jnp...  6.04 us
    while x1, local copies, waits for them, and re-layouts, band_quadratic(): return lax.map(one_band, matrices)  2.92 us
  transfers between devices with their start and end apart: 1, of which 0 were waited for; matrix products, arithmetic and copies ran while one was open for 1% of the time, Pallas kernels for 0%

profile of v1, /device:TPU:0, one launch (start us, length us, event | category | flops | bytes accessed | tf_op | source)
XLA Modules:
  0.0 117.7 jit_solution(12229999035581839562)
XLA Ops:
  7.2 0.8 divide_select_fusion
  8.0 6.0 %convolution_convert_fusion = bf16[8,64,512]{2,1,0:T(8,128)(2,1)} fusion(bf16[8,1024,512]{2,1,0:T(8,128)(2,1)} %param.9, bf16[8,64,1024]{2,1,0:T(8,128)(2,1)} %param.7, f32[8,1024]{1,0:T(8,128)S(1)} %divide_select_fusion), kind=kOutput, calls=%fused_computation.6 | convolution fusion | flops 538705920 | bytes 9994240 | tf_op jit(solution)/shard_map/msi,miw->msw/dot_general | solution.py:15
  14.1 0.6 reduce_sum.44
  15.4 0.1 dynamic-update-slice
  15.5 42.2 %all-reduce = f32[32]{0:T(128)S(1)} all-reduce(f32[32]{0:T(128)S(1)} %dynamic-update-slice), channel_id=1, replica_groups=mesh['ma'=8,'band'=4] {'ma','band'}, use_global_device_ids=true, to_apply=%add | all-reduce | flops 32 | bytes 256
  57.8 0.6 reduce_sum.45
  58.4 2.9 %copy.9 = bf16[2048,512]{0,1:T(8,128)(2,1)S(1)} copy(bf16[2048,512]{1,0:T(8,128)(2,1)} %bitcast.22) | data formatting | bytes 4194304 | tf_op jit(solution)/shard_map/while | solution.py:26
  61.3 26.5 %while.10 = (s32[]{:T(128)}, f32[10,32]{1,0:T(8,128)S(1)}, bf16[10,512,512]{2,1,0:T(8,128)(2,1)}, bf16[2048,512]{0,1:T(8,128)(2,1)S(1)}, s32[]{:T(128)}, /*index=5*/f32[]{:T(128)}, s32[]{:T(128)}) while((s32[]{:T(128)}, f32[10,32]{1,0:T(8,128)S(1)}, bf16[10,512,512]{2,1,0:T(8,128)(2,1)}, bf16[2048,512]{0,1:T(8,128)(2,1)S(1)}, s32[]{:T(128)}, ...), condition=%wide.region_3.4_spmd, body=%wide.region_0.3_spmd.sunk | while | flops 1076887552 | bytes 4752341 | solution.py:26
  61.3 2.4 %fusion.12 = f32[2048]{0:T(1024)S(1)} fusion(bf16[2048,512]{0,1:T(8,128)(2,1)S(1)} %get-tuple-element.89, bf16[10,512,512]{2,1,0:T(8,128)(2,1)} %get-tuple-element.88, s32[]{:T(128)} %get-tuple-element.79), kind=kOutput, calls=%fused_computation.1.clone.1 | convolution fusion | flops 1076885504 | bytes 4727296 | tf_op jit(solution)/shard_map/while/body/eval_jaxpr/dot_general | solution.py:23
  63.8 0.1 reduce_sum.52
  63.8 0.1 reduce_sum.53
  64.0 2.4 %fusion.12 = f32[2048]{0:T(1024)S(1)} fusion(bf16[2048,512]{0,1:T(8,128)(2,1)S(1)} %get-tuple-element.89, bf16[10,512,512]{2,1,0:T(8,128)(2,1)} %get-tuple-element.88, s32[]{:T(128)} %get-tuple-element.79), kind=kOutput, calls=%fused_computation.1.clone.1 | convolution fusion | flops 1076885504 | bytes 4727296 | tf_op jit(solution)/shard_map/while/body/eval_jaxpr/dot_general | solution.py:23
  66.5 0.1 reduce_sum.53
  66.6 2.4 %fusion.12 = f32[2048]{0:T(1024)S(1)} fusion(bf16[2048,512]{0,1:T(8,128)(2,1)S(1)} %get-tuple-element.89, bf16[10,512,512]{2,1,0:T(8,128)(2,1)} %get-tuple-element.88, s32[]{:T(128)} %get-tuple-element.79), kind=kOutput, calls=%fused_computation.1.clone.1 | convolution fusion | flops 1076885504 | bytes 4727296 | tf_op jit(solution)/shard_map/while/body/eval_jaxpr/dot_general | solution.py:23
  69.1 0.1 reduce_sum.53
  69.3 2.4 %fusion.12 = f32[2048]{0:T(1024)S(1)} fusion(bf16[2048,512]{0,1:T(8,128)(2,1)S(1)} %get-tuple-element.89, bf16[10,512,512]{2,1,0:T(8,128)(2,1)} %get-tuple-element.88, s32[]{:T(128)} %get-tuple-element.79), kind=kOutput, calls=%fused_computation.1.clone.1 | convolution fusion | flops 1076885504 | bytes 4727296 | tf_op jit(solution)/shard_map/while/body/eval_jaxpr/dot_general | solution.py:23
  71.8 0.1 reduce_sum.53
  71.9 2.4 %fusion.12 = f32[2048]{0:T(1024)S(1)} fusion(bf16[2048,512]{0,1:T(8,128)(2,1)S(1)} %get-tuple-element.89, bf16[10,512,512]{2,1,0:T(8,128)(2,1)} %get-tuple-element.88, s32[]{:T(128)} %get-tuple-element.79), kind=kOutput, calls=%fused_computation.1.clone.1 | convolution fusion | flops 1076885504 | bytes 4727296 | tf_op jit(solution)/shard_map/while/body/eval_jaxpr/dot_general | solution.py:23
  74.4 0.1 reduce_sum.53
  74.6 2.4 %fusion.12 = f32[2048]{0:T(1024)S(1)} fusion(bf16[2048,512]{0,1:T(8,128)(2,1)S(1)} %get-tuple-element.89, bf16[10,512,512]{2,1,0:T(8,128)(2,1)} %get-tuple-element.88, s32[]{:T(128)} %get-tuple-element.79), kind=kOutput, calls=%fused_computation.1.clone.1 | convolution fusion | flops 1076885504 | bytes 4727296 | tf_op jit(solution)/shard_map/while/body/eval_jaxpr/dot_general | solution.py:23
  77.1 0.1 reduce_sum.53
  77.3 2.4 %fusion.12 = f32[2048]{0:T(1024)S(1)} fusion(bf16[2048,512]{0,1:T(8,128)(2,1)S(1)} %get-tuple-element.89, bf16[10,512,512]{2,1,0:T(8,128)(2,1)} %get-tuple-element.88, s32[]{:T(128)} %get-tuple-element.79), kind=kOutput, calls=%fused_computation.1.clone.1 | convolution fusion | flops 1076885504 | bytes 4727296 | tf_op jit(solution)/shard_map/while/body/eval_jaxpr/dot_general | solution.py:23
  79.7 0.1 reduce_sum.53
  79.9 2.4 %fusion.12 = f32[2048]{0:T(1024)S(1)} fusion(bf16[2048,512]{0,1:T(8,128)(2,1)S(1)} %get-tuple-element.89, bf16[10,512,512]{2,1,0:T(8,128)(2,1)} %get-tuple-element.88, s32[]{:T(128)} %get-tuple-element.79), kind=kOutput, calls=%fused_computation.1.clone.1 | convolution fusion | flops 1076885504 | bytes 4727296 | tf_op jit(solution)/shard_map/while/body/eval_jaxpr/dot_general | solution.py:23
  82.4 0.1 reduce_sum.53
  82.6 2.4 %fusion.12 = f32[2048]{0:T(1024)S(1)} fusion(bf16[2048,512]{0,1:T(8,128)(2,1)S(1)} %get-tuple-element.89, bf16[10,512,512]{2,1,0:T(8,128)(2,1)} %get-tuple-element.88, s32[]{:T(128)} %get-tuple-element.79), kind=kOutput, calls=%fused_computation.1.clone.1 | convolution fusion | flops 1076885504 | bytes 4727296 | tf_op jit(solution)/shard_map/while/body/eval_jaxpr/dot_general | solution.py:23
  85.0 0.1 reduce_sum.53
  85.2 2.4 %fusion.12 = f32[2048]{0:T(1024)S(1)} fusion(bf16[2048,512]{0,1:T(8,128)(2,1)S(1)} %get-tuple-element.89, bf16[10,512,512]{2,1,0:T(8,128)(2,1)} %get-tuple-element.88, s32[]{:T(128)} %get-tuple-element.79), kind=kOutput, calls=%fused_computation.1.clone.1 | convolution fusion | flops 1076885504 | bytes 4727296 | tf_op jit(solution)/shard_map/while/body/eval_jaxpr/dot_general | solution.py:23
  87.7 0.1 reduce_sum.53
  87.9 0.7 multiply_reduce_fusion
  88.6 21.1 %psum.7 = f32[10]{0:T(128)S(1)} all-reduce(f32[10]{0:T(128)S(1)} %get-tuple-element.45), channel_id=1, replica_groups=mesh['ma'=8,'band'=4] {'ma'}, use_global_device_ids=true, to_apply=%region_5.6 | all-reduce | flops 10 | bytes 80 | tf_op jit(solution)/shard_map/psum | solution.py:40
  109.7 1.1 multiply_divide_fusion
  (26 shorter events, 1.0 us)
Async XLA Ops:
  7.2 51.2 %all-gather.2.cloned.1.call-start = ((), (), s32[]{:S(2)}) async-start(), calls=%async_computation | async-start | bytes 2621440 | tf_op jit(solution)/shard_map/all_gather | solution.py:37
  8.0 6.1 %copy-start = (s32[8]{0:T(128)S(1)}, s32[8]{0:T(128)}, u32[]{:S(2)}) copy-start(s32[8]{0:T(128)} %param.11) | copy-start | bytes 100
Sparse Core Ops, SparseCore 0:
  14.2 25.4 all-gather.1
